TPU v7x, 128 devices: a whole 4x4x4 slice. The times are simulated.
128 devices in a mesh: seq: 16 (over x_lo, z, core), head: 4 (over y), batch: 2 (over x_hi).
Axes of the slice: x: 4 (x_hi: 2, x_lo: 2; x = x_hi * 2 + x_lo), y: 4, z: 4, core: 2. Of those that a mesh axis runs over, the one named last changes fastest.
Arguments:
- tokens: bfloat16 [32768, 2048], P(('batch', 'seq')), parts along dimension 0, may hold values from -6 to 6
- neighbor_bank: bfloat16 [512, 256, 2048], P(('batch', 'seq')), parts along dimension 0, may hold values from -2100 to 2100
- slots: int32 [512], P(('batch', 'seq')), parts along dimension 0, may hold values from 0 to 15
- w_query: bfloat16 [2048, 2048], P('seq', 'head'), may hold values from -0.125 to 0.125
- w_key: bfloat16 [2048, 2048], P('seq', 'head'), may hold values from -0.125 to 0.125
- w_value: bfloat16 [2048, 2048], P('seq', 'head'), may hold values from -0.125 to 0.125
- w_out: bfloat16 [2048, 2048], P('head', 'seq'), may hold values from -0.125 to 0.125
Outputs:
- cross_out: bfloat16 [32768, 2048], P(('batch', 'seq'), 'head'), parts along dimension 0
There are 2 independent parts, one for each index of `batch`. A program takes and returns all parts, laid end to end along the dimension named above; an argument that names none is the same for every part. Nothing has to cross between parts.
Inputs may be any that keep to these rules, and one draw needn't show every extreme that they name: Entry c picks row c // 16 * 16 + slots[c] of neighbor_bank.
All inputs are finite; a program needn't handle non-finite values.
Results may differ from a plain program's by a relative error of at most 0.006.
The roundings to bfloat16 on the way count: a program that leaves them out, or rounds other values in their place, can miss the bound.
Values may be sent and summed in bfloat16 or wider, within the bound.
No kernel may reach another device: no remote copies, remote signals or barrier semaphores. Data moves between devices by JAX's collectives and lax.ppermute only.
A program may use at most 128 MiB of HBM per device.

v0:
```python
import math
import jax
import jax.numpy as jnp
from jax import lax
from jax.sharding import PartitionSpec as P

HEAD_DIM = 128


def passed_along(block, axis, distance):
    devices = range(lax.axis_size(axis))
    route = [(i - distance, i) for i in devices if i - distance in devices]
    return lax.ppermute(block, axis, route)


def side_by_side(arrays, axis, dim, along):
    ends, at = ([], 0)
    for a in arrays[:-1]:
        at += a.shape[along]
        ends.append(at)
    both = jnp.concatenate(arrays, axis=along)
    return tuple(jnp.split(lax.all_gather(both, axis, axis=dim, tiled=True), ends, axis=along))


def attend(query_blocks, key_blocks, value_blocks):
    scores = jnp.einsum(
        "cmhd,cnhd->chmn", query_blocks, key_blocks, preferred_element_type=jnp.float32
    ) / math.sqrt(HEAD_DIM)
    peak_score = jnp.max(scores, axis=-1, keepdims=True)
    exponent = jnp.exp(scores - peak_score)
    weights = (exponent / jnp.sum(exponent, axis=-1, keepdims=True)).astype(jnp.bfloat16)
    blended = jnp.einsum(
        "chmn,cnhd->cmhd", weights, value_blocks, preferred_element_type=jnp.float32
    ).astype(jnp.bfloat16)
    return blended.reshape(blended.shape[0] * blended.shape[1], blended.shape[2] * blended.shape[3])


def fold_rows(source, shard_rows):
    return jnp.dot(source, shard_rows, preferred_element_type=jnp.float32)


def local(tokens, neighbor_bank, slots, w_query, w_key, w_value, w_out):
    tok_rows, model_width = tokens.shape
    block_count = neighbor_bank.shape[0]
    neighbor_rows = neighbor_bank.shape[1]
    block_len = tok_rows // block_count
    local_width = w_query.shape[1]
    local_heads = local_width // HEAD_DIM
    hidden = tokens.astype(jnp.float32)
    normed = (hidden * lax.rsqrt(jnp.mean(hidden * hidden, axis=-1, keepdims=True) + 1e-06)).astype(
        jnp.bfloat16
    )
    retrieved = jnp.take(neighbor_bank, slots, axis=0)
    arrived = passed_along(retrieved[block_count - 1], "seq", 1)
    context = jnp.concatenate([arrived[None], retrieved[: block_count - 1]], axis=0)
    context_flat = context.reshape(block_count * neighbor_rows, model_width)
    shard_rows = side_by_side((w_query, w_key, w_value), "seq", 0, 1)
    query_sum = fold_rows(normed, shard_rows[0])
    key_sum = fold_rows(context_flat, shard_rows[1])
    value_sum = fold_rows(context_flat, shard_rows[2])
    query_blocks = query_sum.astype(jnp.bfloat16).reshape(
        block_count, block_len, local_heads, HEAD_DIM
    )
    key_blocks = key_sum.astype(jnp.bfloat16).reshape(
        block_count, neighbor_rows, local_heads, HEAD_DIM
    )
    value_blocks = value_sum.astype(jnp.bfloat16).reshape(
        block_count, neighbor_rows, local_heads, HEAD_DIM
    )
    attended = attend(query_blocks, key_blocks, value_blocks)
    every_head = lax.all_gather(attended, "head", axis=1, tiled=True)
    wide_rows = lax.all_gather(w_out, "seq", axis=1, tiled=True)
    own_columns = lax.all_to_all(wide_rows, "head", split_axis=1, concat_axis=0, tiled=True)
    return jnp.dot(every_head, own_columns, preferred_element_type=jnp.float32).astype(jnp.bfloat16)


def solution(mesh):
    in_specs = (
        P(("batch", "seq"), None),
        P(("batch", "seq"), None, None),
        P(("batch", "seq")),
        P("seq", "head"),
        P("seq", "head"),
        P("seq", "head"),
        P("head", "seq"),
    )
    out_specs = P(("batch", "seq"), "head")
    return jax.shard_map(local, mesh=mesh, in_specs=in_specs, out_specs=out_specs, check_vma=False)
```

profile of v0, /device:TPU:3, one launch (start us, length us, event | category | flops | bytes accessed | tf_op | source)
XLA Modules:
  0.0 214.9 jit_solution(9233872285534013376)
XLA Ops:
  6.5 1.8 pad_maximum_fusion.1
  8.3 0.0 all-gather.4.cloned.1.call-update
  8.4 0.0 all-gather.8.cloned.1.call-start
  8.4 0.7 compare_select_fusion
  9.1 13.1 %gather_fusion = bf16[16,256,2048]{2,1,0:T(8,128)(2,1)} fusion(bf16[16,256,2048]{2,1,0:T(8,128)(2,1)} %param.8, s32[1024]{0:T(1024)S(1)} %pad_clamp_fusion), kind=kCustom, calls=%fused_computation | custom fusion | bytes 33554496 | tf_op jit(solution)/shard_map/jit(_take)/gather | solution.py:53
  22.2 8.7 %broadcast_select_fusion = bf16[16,256,2048]{2,1,0:T(8,128)(2,1)S(1)} fusion(bf16[16,256,2048]{2,1,0:T(8,128)(2,1)} %gather_fusion, pred[16]{0:T(512)(128)(4,1)S(1)} %compare_and_fusion), kind=kLoop, calls=%fused_computation.3 | loop fusion | flops 8388608 | bytes 33554448 | tf_op jit(solution)/shard_map/jit(_take)/select_n | solution.py:53
  31.0 5.9 %copy-done = bf16[16,256,2048]{2,1,0:T(8,128)(2,1)} copy-done((bf16[16,256,2048]{2,1,0:T(8,128)(2,1)}, bf16[16,256,2048]{2,1,0:T(8,128)(2,1)S(1)}, u32[]{:S(2)}) %copy-start) | copy-done | bytes 16777240
  36.9 0.1 slice_bitcast_fusion
  37.0 4.1 %collective-permute-start = (bf16[256,2048]{1,0:T(8,128)(2,1)S(1)}, bf16[256,2048]{1,0:T(8,128)(2,1)S(1)}, u32[]{:S(2)}, u32[]{:S(2)}) collective-permute-start(bf16[256,2048]{1,0:T(8,128)(2,1)S(1)} %slice_bitcast_fusion), channel_id=1, source_target_pairs={{0,8},{8,16},{16,24},{24,32},{32,40},{40,48},{48,56},{56,64},{64,7... | collective-permute-start | bytes 3145736 | tf_op jit(solution)/shard_map/ppermute | solution.py:13
  41.1 0.8 copy.19
  41.9 0.0 all-gather.6.cloned.1.call-start
  42.0 2.2 %copy-done.1 = bf16[1024,2048]{1,0:T(8,128)(2,1)S(1)} copy-done((bf16[1024,2048]{1,0:T(8,128)(2,1)S(1)}, bf16[1024,2048]{1,0:T(8,128)(2,1)}, u32[]{:S(2)}) %copy-start.1) | copy-done | bytes 4194328
  44.2 0.9 fusion.1
  45.1 16.4 %collective-permute-done = bf16[256,2048]{1,0:T(8,128)(2,1)S(1)} collective-permute-done((bf16[256,2048]{1,0:T(8,128)(2,1)S(1)}, bf16[256,2048]{1,0:T(8,128)(2,1)S(1)}, u32[]{:S(2)}, u32[]{:S(2)}) %collective-permute-start) | collective-permute-done | bytes 1048608 | tf_op jit(solution)/shard_map/ppermute | solution.py:13
  61.5 6.4 %pad_maximum_fusion = bf16[16,256,2048]{2,1,0:T(8,128)(2,1)} fusion(bf16[15,256,2048]{2,1,0:T(8,128)(2,1)S(1)} %slice-done, bf16[1,256,2048]{2,1,0:T(8,128)(2,1)S(1)} %bitcast.25), kind=kLoop, calls=%fused_computation.2 | loop fusion | flops 8388608 | bytes 33554432 | tf_op jit(solution)/shard_map/concatenate | solution.py:55
  68.0 14.5 %convolution_convert_fusion = bf16[4096,512]{1,0:T(8,128)(2,1)} fusion(bf16[4096,2048]{1,0:T(8,128)(2,1)} %bitcast.18, bf16[2048,1536]{1,0:T(8,128)(2,1)} %all-gather.4.cloned.1.call-done), kind=kOutput, calls=%fused_computation.8 | convolution fusion | flops 8592031744 | bytes 23068672 | tf_op jit(solution)/shard_map/dot_general | solution.py:39
  82.4 7.0 %reshape.36 = bf16[16,256,4,128]{3,2,1,0:T(4,128)(2,1)} reshape(bf16[4096,512]{1,0:T(8,128)(2,1)} %convolution_convert_fusion) | data formatting | bytes 8388608 | tf_op jit(solution)/shard_map/reshape | solution.py:64
  89.4 5.2 %fusion.21 = bf16[1024,512]{1,0:T(8,128)(2,1)S(1)} fusion(bf16[2048,1536]{1,0:T(8,128)(2,1)} %all-gather.4.cloned.1.call-done, bf16[1024,2048]{1,0:T(8,128)(2,1)} %param.7, f32[1024]{0:T(1024)S(1)} %add_rsqrt_fusion), kind=kOutput, calls=%fused_computation.26 | convolution fusion | flops 2154299392 | bytes 7344128 | tf_op jit(solution)/shard_map/dot_general | solution.py:39
  94.6 0.3 reshape.35
  94.9 14.4 %convolution_convert_fusion.1 = bf16[4096,512]{1,0:T(8,128)(2,1)} fusion(bf16[4096,2048]{1,0:T(8,128)(2,1)} %bitcast.19, bf16[2048,1536]{1,0:T(8,128)(2,1)} %all-gather.4.cloned.1.call-done), kind=kOutput, calls=%fused_computation.9 | convolution fusion | flops 8592031744 | bytes 23068672 | tf_op jit(solution)/shard_map/dot_general | solution.py:39
  109.3 6.9 %reshape.34 = bf16[16,256,4,128]{3,2,1,0:T(4,128)(2,1)} reshape(bf16[4096,512]{1,0:T(8,128)(2,1)} %convolution_convert_fusion.1) | data formatting | bytes 8388608 | tf_op jit(solution)/shard_map/reshape | solution.py:67
  116.2 3.8 %fusion.7 = f32[16,4,64,256]{3,2,1,0:T(8,128)S(1)} fusion(bf16[16,256,4,128]{3,2,1,0:T(4,128)(2,1)} %reshape.36, bf16[16,64,4,128]{3,2,1,0:T(4,128)(2,1)S(1)} %reshape.35), kind=kOutput, calls=%fused_computation.13 | convolution fusion | flops 268435456 | bytes 9437184 | tf_op jit(solution)/shard_map/cmhd,cnhd->chmn/dot_general | solution.py:26
  120.0 2.0 copy-done.2
  122.0 1.6 fusion.38
  123.6 11.9 %fusion.26 = bf16[16,64,4,128]{3,1,2,0:T(8,128)(2,1)S(1)} fusion(bf16[16,256,4,128]{3,2,1,0:T(4,128)(2,1)} %reshape.34, f32[16,4,64]{2,1,0:T(4,128)S(1)} %fusion.38, f32[16,4,64,256]{3,2,1,0:T(8,128)} %copy-done.2), kind=kOutput, calls=%fused_computation.28 | convolution fusion | flops 274206976 | bytes 9453568 | tf_op jit(solution)/shard_map/chmn,cnhd->cmhd/dot_general | solution.py:32
  135.5 0.9 copy.18
  136.4 1.2 copy.33
  137.6 0.0 all-gather.8.cloned.1.call-done
  137.6 35.9 %all_to_all.19 = bf16[512,4,512]{0,2,1:T(8,128)(2,1)S(1)} all-to-all(bf16[512,4,512]{0,2,1:T(8,128)(2,1)} %bitcast.23), channel_id=1, replica_groups=mesh['seq'=16,'head'=4,'batch'=2] {'head'}, dimensions={1} | all-to-all | bytes 4194304 | tf_op jit(solution)/shard_map/all_to_all | solution.py:73
  173.5 2.4 %copy.20 = bf16[4,512,512]{2,1,0:T(8,128)(2,1)} copy(bf16[4,512,512]{1,2,0:T(8,128)(2,1)S(1)} %bitcast.20) | data formatting | bytes 4194304 | tf_op jit(solution)/shard_map/all_to_all | solution.py:73
  175.9 26.3 %all-gather.6.cloned.1.call-done = bf16[1024,2048]{1,0:T(8,128)(2,1)} async-done(((bf16[1024,512]{1,0:T(8,128)(2,1)}), bf16[1024,2048]{1,0:T(8,128)(2,1)}) %all-gather.6.cloned.1.call-update) | async-done | bytes 4194320 | tf_op jit(solution)/shard_map/all_gather | solution.py:71
  202.2 6.2 %convolution_convert_fusion.2 = bf16[1024,512]{1,0:T(8,128)(2,1)} fusion(bf16[1024,2048]{1,0:T(8,128)(2,1)} %all-gather.6.cloned.1.call-done, bf16[2048,512]{1,0:T(8,128)(2,1)} %bitcast.24), kind=kOutput, calls=%fused_computation.27 | convolution fusion | flops 2148007936 | bytes 7340032 | tf_op jit(solution)/shard_map/dot_general | solution.py:74
  (16 shorter events, 0.1 us)
Async XLA Ops:
  6.5 61.4 %all-gather.4.cloned.1.call-start = ((), (), s32[]{:S(2)}) async-start(), calls=%async_computation.1 | async-start | bytes 6684672 | tf_op jit(solution)/shard_map/all_gather | solution.py:22
  8.4 129.2 %all-gather.8.cloned.1.call-start = ((), (), s32[]{:S(2)}) async-start(), calls=%async_computation.3 | async-start | bytes 2228224 | tf_op jit(solution)/shard_map/all_gather | solution.py:72
  9.1 13.1 %copy-start.4 = (s32[16]{0:T(128)S(1)}, s32[16]{0:T(128)}, u32[]{:S(2)}) copy-start(s32[16]{0:T(128)} %param.9) | copy-start | bytes 196
  22.2 18.9 %copy-start.3 = (bf16[512,128]{1,0:T(8,128)(2,1)S(1)}, bf16[512,128]{1,0:T(8,128)(2,1)}, u32[]{:S(2)}) copy-start(bf16[512,128]{1,0:T(8,128)(2,1)} %param.13) | copy-start | bytes 393220
  31.0 5.9 %copy-start = (bf16[16,256,2048]{2,1,0:T(8,128)(2,1)}, bf16[16,256,2048]{2,1,0:T(8,128)(2,1)S(1)}, u32[]{:S(2)}) copy-start(bf16[16,256,2048]{2,1,0:T(8,128)(2,1)S(1)} %broadcast_select_fusion) | copy-start | bytes 50331652
  37.0 24.5 %collective-permute-start = (bf16[256,2048]{1,0:T(8,128)(2,1)S(1)}, bf16[256,2048]{1,0:T(8,128)(2,1)S(1)}, u32[]{:S(2)}, u32[]{:S(2)}) collective-permute-start(bf16[256,2048]{1,0:T(8,128)(2,1)S(1)} %slice_bitcast_fusion), channel_id=1, source_target_pairs={{0,8},{8,16},{16,24},{24,32},{32,40},{40,48},{48,56},{56,64},{64,7... | collective-permute-start | bytes 3145736 | tf_op jit(solution)/shard_map/ppermute | solution.py:13
  41.9 160.2 %all-gather.6.cloned.1.call-start = ((), (), s32[]{:S(2)}) async-start(), calls=%async_computation.2 | async-start | bytes 5242880 | tf_op jit(solution)/shard_map/all_gather | solution.py:71
  42.0 2.3 %copy-start.1 = (bf16[1024,2048]{1,0:T(8,128)(2,1)S(1)}, bf16[1024,2048]{1,0:T(8,128)(2,1)}, u32[]{:S(2)}) copy-start(bf16[1024,2048]{1,0:T(8,128)(2,1)} %param.7) | copy-start | bytes 12582916
  42.0 19.5 %slice-start = ((bf16[16,256,2048]{2,1,0:T(8,128)(2,1)}), bf16[15,256,2048]{2,1,0:T(8,128)(2,1)S(1)}, s32[]{:S(2)}) async-start(bf16[16,256,2048]{2,1,0:T(8,128)(2,1)} %copy-done), calls=%async_computation.4 | async-start | bytes 31457280 | tf_op jit(solution)/shard_map/slice | solution.py:55
  120.0 2.0 copy-start.2
Sparse Core Ops, SparseCore 0:
  9.0 46.2 all-gather.3
  57.0 37.4 all-gather.7
  137.7 64.4 all-gather.5
where the time goes:
time: 216 us; the launch traced here: 215 us
  matrix products  55.9 us (26%)
  waiting for transfers between devices  42.7 us (20%)
  local copies, waits for them, and re-layouts  42.7 us (20%)
  blocking collectives  35.9 us (17%)
  other arithmetic  20.2 us (9%)
  between operations  13.2 us (6%)
  starting transfers between devices  4.22 us (2%)
    all_to_all x1, blocking collectives, local(): lax.all_to_all(wide_rows, 'head', split_axis=1, concat_axis=0, tiled=True)  35.9 us
    dot_general x3, matrix products, fold_rows(): return jnp.dot(source, shard_rows, preferred_element_type=jnp.float32)  34.1 us
    all_gather x1, waiting for transfers between devices, local(): every_head = lax.all_gather(attended, 'head', axis=1, tiled=True)  26.3 us
    ppermute x1, waiting for transfers between devices, passed_along(): return lax.ppermute(block, axis, route)  16.4 us
    gather x1, local copies, waits for them, and re-layouts, local(): retrieved = jnp.take(neighbor_bank, slots, axis=0)  13.1 us
    unnamed x12, local copies, waits for them, and re-layouts  12.1 us
    dot_general x1, matrix products, attend(): jnp.einsum('chmn,cnhd->cmhd', weights, value_blocks, preferred_element_ty...  11.9 us
    select_n x2, other arithmetic, local(): retrieved = jnp.take(neighbor_bank, slots, axis=0)  9.4 us
  transfers between devices with their start and end apart: 4, of which 2 were waited for; matrix products, arithmetic and copies ran while one was open for 47% of the time, Pallas kernels for 0%

commit v1 on v0

--- a/solution.py
+++ b/solution.py
@@ -68,7 +68,10 @@
         block_count, neighbor_rows, local_heads, HEAD_DIM
     )
     attended = attend(query_blocks, key_blocks, value_blocks)
-    every_head = lax.all_gather(attended, "head", axis=1, tiled=True)
+    axis_n = jax.lax.psum(1, "head")
+    arrivals = tuple((axis_n if hop_no == 1 else 1 for hop_no in range(attended.ndim)))
+    block_last = jnp.tile(attended, arrivals)
+    every_head = jax.lax.all_to_all(block_last, "head", split_axis=1, concat_axis=1, tiled=True)
     wide_rows = lax.all_gather(w_out, "seq", axis=1, tiled=True)
     own_columns = lax.all_to_all(wide_rows, "head", split_axis=1, concat_axis=0, tiled=True)
     return jnp.dot(every_head, own_columns, preferred_element_type=jnp.float32).astype(jnp.bfloat16)

time: 216 us -> 224 us (1.037)
  blocking collectives: 35.9 us -> 51.8 us
  waiting for transfers between devices: 42.7 us -> 35.5 us
  starting transfers between devices: 4.22 us -> 8.52 us
  local copies, waits for them, and re-layouts: 42.7 us -> 39.5 us
  matrix products: 55.9 us -> 52.8 us
    all_gather x1 -> x0, waiting for transfers between devices: 26.3 us -> none  [local(): every_head = lax.all_gather(attended, 'head', axis=1, tiled=True)]
    all_gather x1, waiting for transfers between devices: 0.01 us -> 25.1 us  [side_by_side(): lax.all_gather(both, axis, axis=dim, tiled=True)]
    all_to_all x1, blocking collectives: 35.9 us -> 51.8 us  [local(): jax.lax.all_to_all(block_last, 'head', split_axis=1, concat_axis=1, tiled...]
    unnamed x12 -> x10, local copies, waits for them, and re-layouts: 12.1 us -> 3.82 us
    ppermute x1, waiting for transfers between devices: 16.4 us -> 10.4 us  [passed_along(): return lax.ppermute(block, axis, route)]
    all_to_all x0 -> x1, starting transfers between devices: none -> 4.17 us  [local(): lax.all_to_all(wide_rows, 'head', split_axis=1, concat_axis=0, tiled=True)]
    dot_general x1, matrix products: 6.16 us -> 3.29 us  [local(): jnp.dot(every_head, own_columns, preferred_element_type=jnp.float32)]
where the time goes in v1:
time: 224 us; the launch traced here: 222 us
  matrix products  52.8 us (24%)
  blocking collectives  51.8 us (23%)
  local copies, waits for them, and re-layouts  39.5 us (18%)
  waiting for transfers between devices  35.5 us (16%)
  other arithmetic  20.1 us (9%)
  between operations  13.5 us (6%)
  starting transfers between devices  8.52 us (4%)
    all_to_all x1, blocking collectives, local(): jax.lax.all_to_all(block_last, 'head', split_axis=1, concat_axis=1, tiled...  51.8 us
    dot_general x3, matrix products, fold_rows(): return jnp.dot(source, shard_rows, preferred_element_type=jnp.float32)  33.8 us
    all_gather x1, waiting for transfers between devices, side_by_side(): lax.all_gather(both, axis, axis=dim, tiled=True)  25.1 us
    gather x1, local copies, waits for them, and re-layouts, local(): retrieved = jnp.take(neighbor_bank, slots, axis=0)  13.1 us
    dot_general x1, matrix products, attend(): jnp.einsum('chmn,cnhd->cmhd', weights, value_blocks, preferred_element_ty...  11.9 us
    ppermute x1, waiting for transfers between devices, passed_along(): return lax.ppermute(block, axis, route)  10.4 us
    select_n x2, other arithmetic, local(): retrieved = jnp.take(neighbor_bank, slots, axis=0)  9.33 us
    reshape x1, local copies, waits for them, and re-layouts, local(): key_sum.astype(jnp.bfloat16)  6.94 us
  transfers between devices with their start and end apart: 4, of which 2 were waited for; matrix products, arithmetic and copies ran while one was open for 47% of the time, Pallas kernels for 0%

profile of v1, /device:TPU:3, one launch (start us, length us, event | category | flops | bytes accessed | tf_op | source)
XLA Modules:
  0.0 221.9 jit_solution(3954884274622827346)
XLA Ops:
  6.5 1.7 copy.15
  8.2 0.0 all-gather.5.cloned.1.call-update
  8.2 0.0 all-gather.3.cloned.1.call-start
  8.3 1.8 pad_maximum_fusion.1
  10.1 0.0 all-gather.3.cloned.1.call-update
  10.1 0.7 compare_select_fusion
  10.8 13.1 %gather_fusion = bf16[16,256,2048]{2,1,0:T(8,128)(2,1)} fusion(bf16[16,256,2048]{2,1,0:T(8,128)(2,1)} %param.8, s32[1024]{0:T(1024)S(1)} %pad_clamp_fusion), kind=kCustom, calls=%fused_computation | custom fusion | bytes 33554496 | tf_op jit(solution)/shard_map/jit(_take)/gather | solution.py:53
  23.9 8.7 %broadcast_select_fusion = bf16[16,256,2048]{2,1,0:T(8,128)(2,1)S(1)} fusion(bf16[16,256,2048]{2,1,0:T(8,128)(2,1)} %gather_fusion, pred[16]{0:T(512)(128)(4,1)S(1)} %compare_and_fusion), kind=kLoop, calls=%fused_computation.3 | loop fusion | flops 8388608 | bytes 33554448 | tf_op jit(solution)/shard_map/jit(_take)/select_n | solution.py:53
  32.6 0.1 slice_bitcast_fusion
  32.7 4.3 %collective-permute-start = (bf16[256,2048]{1,0:T(8,128)(2,1)S(1)}, bf16[256,2048]{1,0:T(8,128)(2,1)S(1)}, u32[]{:S(2)}, u32[]{:S(2)}) collective-permute-start(bf16[256,2048]{1,0:T(8,128)(2,1)S(1)} %slice_bitcast_fusion), channel_id=1, source_target_pairs={{0,8},{8,16},{16,24},{24,32},{32,40},{40,48},{48,56},{56,64},{64,7... | collective-permute-start | bytes 3145736 | tf_op jit(solution)/shard_map/ppermute | solution.py:13
  37.0 1.8 slice.11
  38.9 0.9 fusion.1
  39.8 10.4 %collective-permute-done = bf16[256,2048]{1,0:T(8,128)(2,1)S(1)} collective-permute-done((bf16[256,2048]{1,0:T(8,128)(2,1)S(1)}, bf16[256,2048]{1,0:T(8,128)(2,1)S(1)}, u32[]{:S(2)}, u32[]{:S(2)}) %collective-permute-start) | collective-permute-done | bytes 1048608 | tf_op jit(solution)/shard_map/ppermute | solution.py:13
  50.2 6.5 %pad_maximum_fusion = bf16[16,256,2048]{2,1,0:T(8,128)(2,1)} fusion(bf16[15,256,2048]{2,1,0:T(8,128)(2,1)S(1)} %slice.11, bf16[1,256,2048]{2,1,0:T(8,128)(2,1)S(1)} %bitcast.27), kind=kLoop, calls=%fused_computation.2 | loop fusion | flops 8388608 | bytes 33554432 | tf_op jit(solution)/shard_map/concatenate | solution.py:55
  56.6 4.2 %copy.16 = bf16[512,4,512]{2,0,1:T(8,128)(2,1)} copy(bf16[512,4,512]{0,2,1:T(8,128)(2,1)} %bitcast.26) | data formatting | bytes 4194304 | tf_op jit(solution)/shard_map/all_to_all | solution.py:76
  60.9 4.2 %all-to-all-start.1 = ((bf16[512,4,512]{2,0,1:T(8,128)(2,1)}), bf16[512,4,512]{2,0,1:T(8,128)(2,1)S(1)}, u32[]{:S(2)}, u32[]{:S(2)}) async-start(bf16[512,4,512]{2,0,1:T(8,128)(2,1)} %copy.16), calls=%async_computation.1 | async-start | bytes 4194304 | tf_op jit(solution)/shard_map/all_to_all | solution.py:76
  65.0 25.1 %all-gather.3.cloned.1.call-done = bf16[2048,1536]{1,0:T(8,128)(2,1)} async-done(((bf16[128,1536]{1,0:T(8,128)(2,1)}), bf16[2048,1536]{1,0:T(8,128)(2,1)}) %all-gather.3.cloned.1.call-update) | async-done | bytes 6291472 | tf_op jit(solution)/shard_map/all_gather | solution.py:22
  90.2 14.4 %convolution_convert_fusion = bf16[4096,512]{1,0:T(8,128)(2,1)} fusion(bf16[4096,2048]{1,0:T(8,128)(2,1)} %bitcast.22, bf16[2048,1536]{1,0:T(8,128)(2,1)} %all-gather.3.cloned.1.call-done), kind=kOutput, calls=%fused_computation.8 | convolution fusion | flops 8592031744 | bytes 23068672 | tf_op jit(solution)/shard_map/dot_general | solution.py:39
  104.6 6.9 %reshape.40 = bf16[16,256,4,128]{3,2,1,0:T(4,128)(2,1)} reshape(bf16[4096,512]{1,0:T(8,128)(2,1)} %convolution_convert_fusion) | data formatting | bytes 8388608 | tf_op jit(solution)/shard_map/reshape | solution.py:64
  111.5 14.5 %convolution_convert_fusion.1 = bf16[4096,512]{1,0:T(8,128)(2,1)} fusion(bf16[4096,2048]{1,0:T(8,128)(2,1)} %bitcast.23, bf16[2048,1536]{1,0:T(8,128)(2,1)} %all-gather.3.cloned.1.call-done), kind=kOutput, calls=%fused_computation.9 | convolution fusion | flops 8592031744 | bytes 23068672 | tf_op jit(solution)/shard_map/dot_general | solution.py:39
  126.0 4.9 %fusion.23 = bf16[1024,512]{1,0:T(8,128)(2,1)} fusion(bf16[2048,1536]{1,0:T(8,128)(2,1)} %all-gather.3.cloned.1.call-done, bf16[1024,2048]{1,0:T(8,128)(2,1)S(1)} %copy-done.1, f32[1024]{0:T(1024)S(1)} %add_rsqrt_fusion), kind=kOutput, calls=%fused_computation.29 | convolution fusion | flops 2154299392 | bytes 7344128 | tf_op jit(solution)/shard_map/dot_general | solution.py:39
  131.0 1.3 reshape.39
  132.3 6.9 %reshape.38 = bf16[16,256,4,128]{3,2,1,0:T(4,128)(2,1)} reshape(bf16[4096,512]{1,0:T(8,128)(2,1)} %convolution_convert_fusion.1) | data formatting | bytes 8388608 | tf_op jit(solution)/shard_map/reshape | solution.py:67
  139.2 3.8 %fusion.7 = f32[16,4,64,256]{3,2,1,0:T(8,128)S(1)} fusion(bf16[16,256,4,128]{3,2,1,0:T(4,128)(2,1)} %reshape.40, bf16[16,64,4,128]{3,2,1,0:T(4,128)(2,1)S(1)} %reshape.39), kind=kOutput, calls=%fused_computation.13 | convolution fusion | flops 268435456 | bytes 9437184 | tf_op jit(solution)/shard_map/cmhd,cnhd->chmn/dot_general | solution.py:26
  143.0 2.0 copy-done.2
  144.9 1.6 fusion.42
  146.6 11.9 %fusion.30 = bf16[16,64,4,128]{3,1,2,0:T(8,128)(2,1)S(1)} fusion(bf16[16,256,4,128]{3,2,1,0:T(4,128)(2,1)} %reshape.38, f32[16,4,64]{2,1,0:T(4,128)S(1)} %fusion.42, f32[16,4,64,256]{3,2,1,0:T(8,128)} %copy-done.2), kind=kOutput, calls=%fused_computation.30 | convolution fusion | flops 274206976 | bytes 9453568 | tf_op jit(solution)/shard_map/chmn,cnhd->cmhd/dot_general | solution.py:32
  158.5 0.9 copy.14
  159.4 0.2 copy.29
  159.6 0.3 tile.9
  159.9 51.8 %all_to_all.22 = bf16[1024,4,512]{2,0,1:T(8,128)(2,1)S(1)} all-to-all(bf16[1024,4,512]{2,0,1:T(8,128)(2,1)S(1)} %tile.9), channel_id=1, replica_groups=mesh['seq'=16,'head'=4,'batch'=2] {'head'}, dimensions={1} | all-to-all | bytes 8388608 | tf_op jit(solution)/shard_map/all_to_all | solution.py:74
  211.7 3.3 %bitcast_convert_fusion = bf16[1024,512]{1,0:T(8,128)(2,1)} fusion(bf16[1024,4,512]{2,0,1:T(8,128)(2,1)S(1)} %all_to_all.22, bf16[512,4,512]{2,0,1:T(8,128)(2,1)S(1)} %all-to-all-done.1), kind=kOutput, calls=%fused_computation.23 | convolution fusion | flops 2148007936 | bytes 7340032 | tf_op jit(solution)/shard_map/dot_general | solution.py:77
  (13 shorter events, 0.0 us)
Async XLA Ops:
  6.5 50.1 %all-gather.5.cloned.1.call-start = ((), (), s32[]{:S(2)}) async-start(), calls=%async_computation.3 | async-start | bytes 2228224 | tf_op jit(solution)/shard_map/all_gather | solution.py:75
  8.2 82.0 %all-gather.3.cloned.1.call-start = ((), (), s32[]{:S(2)}) async-start(), calls=%async_computation.2 | async-start | bytes 6684672 | tf_op jit(solution)/shard_map/all_gather | solution.py:22
  10.8 13.1 %copy-start.3 = (s32[16]{0:T(128)S(1)}, s32[16]{0:T(128)}, u32[]{:S(2)}) copy-start(s32[16]{0:T(128)} %param.9) | copy-start | bytes 196
  32.7 6.2 %copy-start = (bf16[1024,2048]{1,0:T(8,128)(2,1)S(1)}, bf16[1024,2048]{1,0:T(8,128)(2,1)}, u32[]{:S(2)}) copy-start(bf16[1024,2048]{1,0:T(8,128)(2,1)} %param.7) | copy-start | bytes 12582916
  32.7 17.4 %collective-permute-start = (bf16[256,2048]{1,0:T(8,128)(2,1)S(1)}, bf16[256,2048]{1,0:T(8,128)(2,1)S(1)}, u32[]{:S(2)}, u32[]{:S(2)}) collective-permute-start(bf16[256,2048]{1,0:T(8,128)(2,1)S(1)} %slice_bitcast_fusion), channel_id=1, source_target_pairs={{0,8},{8,16},{16,24},{24,32},{32,40},{40,48},{48,56},{56,64},{64,7... | collective-permute-start | bytes 3145736 | tf_op jit(solution)/shard_map/ppermute | solution.py:13
  60.9 98.7 %all-to-all-start.1 = ((bf16[512,4,512]{2,0,1:T(8,128)(2,1)}), bf16[512,4,512]{2,0,1:T(8,128)(2,1)S(1)}, u32[]{:S(2)}, u32[]{:S(2)}) async-start(bf16[512,4,512]{2,0,1:T(8,128)(2,1)} %copy.16), calls=%async_computation.1 | async-start | bytes 4194304 | tf_op jit(solution)/shard_map/all_to_all | solution.py:76
  111.5 14.5 %copy-start.1 = (bf16[1024,2048]{1,0:T(8,128)(2,1)S(1)}, bf16[1024,2048]{1,0:T(8,128)(2,1)}, u32[]{:S(2)}) copy-start(bf16[1024,2048]{1,0:T(8,128)(2,1)} %param.7) | copy-start | bytes 12582916
  143.0 2.0 copy-start.2
Sparse Core Ops, SparseCore 0:
  9.0 36.7 all-gather.4
  47.6 42.5 all-gather.2
